TPU v7x, 32 devices: a whole 2x2x4 slice. The times are simulated.
32 devices in a mesh: row: 8 (over y, x, core), col: 4 (over z).
Axes of the slice: x: 2, y: 2, z: 4, core: 2. Of those that a mesh axis runs over, the one named last changes fastest.
Arguments:
- hidden_in: bfloat16 [4096, 2048], P(('row', 'col')), may hold values from -6 to 6
- first_gain: float32 [2048], replicated, may hold values from 0.25 to 1.75
- query_weight: bfloat16 [2048, 4096], P(None, 'col'), may hold values from -0.125 to 0.125
- key_projection: bfloat16 [2048, 512], replicated, may hold values from -0.125 to 0.125
- value_projection: bfloat16 [2048, 512], replicated, may hold values from -0.125 to 0.125
- out_weight: bfloat16 [4096, 2048], P('col'), may hold values from -0.375 to 0.375
- query_gain: float32 [128], replicated, may hold values from 0.6 to 1.6, as said below
- key_gain: float32 [128], replicated, may hold values from 0.6 to 1.6, as said below
- second_gain: float32 [2048], replicated, may hold values from 0.25 to 1.75
- router_weight: bfloat16 [2048, 32], replicated, may hold values from -2 to 2
- gate_weight: bfloat16 [32, 2048, 768], P(('row', 'col')), may hold values from -0.125 to 0.125
- up_weight: bfloat16 [32, 2048, 768], P(('row', 'col')), may hold values from -0.125 to 0.125
- down_weight: bfloat16 [32, 768, 2048], P(('row', 'col')), may hold values from -0.21875 to 0.21875
- segments: int32 [8, 512], P('row'), may hold values from 0 to 2, never falling along the last dimension, each value on 1 to 480 neighbouring positions
- routes: int32 [4096, 8], P(('row', 'col')), may hold values from 0 to 31, all different within a row; in each aligned block of 128 rows (0 to 127, 128 to 255, ...) at most 36 rows name the same one
- cotangent: bfloat16 [4096, 2048], P(('row', 'col')), may hold values from -6 to 6
Outputs:
- block_out: bfloat16 [4096, 2048], P(('row', 'col'))
- input_grad: bfloat16 [4096, 2048], P(('row', 'col'))
- first_gain_grad: float32 [2048], replicated
- query_weight_grad: float32 [2048, 4096], P(None, 'col')
- key_weight_grad: float32 [2048, 512], replicated
- value_weight_grad: float32 [2048, 512], replicated
- out_weight_grad: float32 [4096, 2048], P('col')
- query_gain_grad: float32 [128], replicated
- key_gain_grad: float32 [128], replicated
- second_gain_grad: float32 [2048], replicated
- router_weight_grad: float32 [2048, 32], replicated
- gate_weight_grad: float32 [32, 2048, 768], P(('row', 'col'))
- up_weight_grad: float32 [32, 2048, 768], P(('row', 'col'))
- down_weight_grad: float32 [32, 768, 2048], P(('row', 'col'))
Inputs may be any that keep to these rules, and one draw needn't show every extreme that they name: In the rows of one device (128 tokens, aligned blocks) no expert is named by more than 36 routes, a bound that some block reaches; a token's 8 routes are different experts. `segments`: in each token group the ids start at 0 and never fall; every sequence has 1 to 480 tokens and one has exactly 480. `query_gain`: positive gains. `key_gain`: positive gains.
All inputs are finite; a program needn't handle non-finite values.
Results may differ from a plain program's by a relative error of at most 0.023.
Values may be sent and summed in bfloat16 or wider, within the bound.
A program may use at most 256 MiB of HBM per device.

v0:
```python
import jax
import jax.numpy as jnp
from jax import lax
from jax.sharding import PartitionSpec as P

QUERY_HEADS = 32
KEY_VALUE_HEADS = 4
HEAD_SIZE = 128
TOP = 8
EPSILON = 1e-06
THETA = 1000000.0
NEGATIVE = -1e30


def norm_rows(values, gain):
    return values * lax.rsqrt(jnp.mean(values * values, axis=-1, keepdims=True) + EPSILON) * gain


def positions(segment_row):
    index = jnp.arange(segment_row.shape[0], dtype=jnp.int32)
    begins = jnp.concatenate([jnp.ones((1,), dtype=jnp.bool_), segment_row[1:] != segment_row[:-1]])
    first = lax.cummax(jnp.where(begins, index, 0), axis=0)
    return index - first


def rope_tables(segment_row):
    half_width = HEAD_SIZE // 2
    freqs = THETA ** (-2.0 * jnp.arange(half_width, dtype=jnp.float32) / HEAD_SIZE)
    angles = positions(segment_row).astype(jnp.float32)[:, None] * freqs[None, :]
    return (jnp.cos(angles)[:, None, :], jnp.sin(angles)[:, None, :])


def head_prep(raw, gain, cosine, sine):
    normed_input = norm_rows(raw, gain)
    half_width = HEAD_SIZE // 2
    lower = normed_input[..., :half_width]
    upper = normed_input[..., half_width:]
    return jnp.concatenate([lower * cosine - upper * sine, upper * cosine + lower * sine], axis=-1)


def route_softmax(chosen):
    top_logit = jnp.max(chosen, axis=1, keepdims=True)
    raised = jnp.exp(chosen - top_logit)
    return raised / jnp.sum(raised, axis=1, keepdims=True)


def allowed_block(segment_row, row_begin, row_end):
    query_index = jnp.arange(row_begin, row_end, dtype=jnp.int32)
    key_index = jnp.arange(0, row_end, dtype=jnp.int32)
    causal = key_index[None, :] <= query_index[:, None]
    same_seq = segment_row[None, :row_end] == segment_row[row_begin:row_end, None]
    return causal & same_seq


def slot_numbers(flat_routes, expert_count):
    onehot = (flat_routes[:, None] == jnp.arange(expert_count, dtype=jnp.int32)[None, :]).astype(
        jnp.int32
    )
    earlier = jnp.cumsum(onehot, axis=0) - onehot
    return jnp.sum(earlier * onehot, axis=1)


def place_head(part_grad, full_shape, column_start):
    return lax.dynamic_update_slice_in_dim(
        jnp.zeros(full_shape, jnp.float32), part_grad, column_start, 1
    )


def trade(parcel):
    return lax.all_to_all(parcel, ("row", "col"), split_axis=0, concat_axis=0, tiled=True)


def shards(
    hidden_in,
    first_gain,
    query_weight,
    key_projection,
    value_projection,
    out_weight,
    query_gain,
    key_gain,
    second_gain,
    router_weight,
    gate_weight,
    up_weight,
    down_weight,
    segments,
    routes,
    cotangent,
):
    tok_rows = hidden_in.shape[0]
    model_width = hidden_in.shape[1]
    resid_in = hidden_in.astype(jnp.float32)
    normed_input, first_pull = jax.vjp(norm_rows, resid_in, first_gain)
    normed_low = normed_input.astype(jnp.bfloat16)
    gathered = lax.all_gather(normed_low, "col", axis=0, tiled=True)
    group_rows = gathered.shape[0]
    segment_row = segments[0]
    cosine, sine = rope_tables(segment_row)
    heads_here = query_weight.shape[1] // HEAD_SIZE
    group_heads = QUERY_HEADS // KEY_VALUE_HEADS
    kv_start = lax.axis_index("col") * heads_here // group_heads * HEAD_SIZE
    key_columns = lax.dynamic_slice_in_dim(key_projection, kv_start, HEAD_SIZE, 1)
    value_columns = lax.dynamic_slice_in_dim(value_projection, kv_start, HEAD_SIZE, 1)
    query_raw = jnp.dot(gathered, query_weight, preferred_element_type=jnp.float32).reshape(
        group_rows, heads_here, HEAD_SIZE
    )
    key_full = jnp.dot(gathered, key_columns, preferred_element_type=jnp.float32)
    value_full = jnp.dot(gathered, value_columns, preferred_element_type=jnp.float32)

    def prep_heads(raw, gain):
        return head_prep(raw, gain, cosine, sine)

    query_rotated, query_pull = jax.vjp(prep_heads, query_raw, query_gain)
    key_rotated, key_pull = jax.vjp(prep_heads, key_full[:, None, :], key_gain)
    query_low = query_rotated.astype(jnp.bfloat16)
    key_low = key_rotated[:, 0, :].astype(jnp.bfloat16)
    value_lowered = value_full.astype(jnp.bfloat16)
    block_rows = max(min(512, group_rows), group_rows // 8)
    score_scale = HEAD_SIZE ** (-0.5)
    pieces_out = []
    log_totals = []
    for row_begin in range(0, group_rows, block_rows):
        row_end = row_begin + block_rows
        scores = (
            jnp.einsum(
                "qhd,kd->hqk",
                query_low[row_begin:row_end],
                key_low[:row_end],
                preferred_element_type=jnp.float32,
            )
            * score_scale
        )
        scores = jnp.where(allowed_block(segment_row, row_begin, row_end)[None], scores, NEGATIVE)
        top_score = jnp.max(scores, axis=-1, keepdims=True)
        raised = jnp.exp(scores - top_score)
        row_total = jnp.sum(raised, axis=-1, keepdims=True)
        softmax_low = (raised / row_total).astype(jnp.bfloat16)
        pieces_out.append(
            jnp.einsum(
                "hqk,kd->qhd",
                softmax_low,
                value_lowered[:row_end],
                preferred_element_type=jnp.float32,
            )
        )
        log_totals.append(top_score + jnp.log(row_total))
    attention_output = (
        jnp.concatenate(pieces_out, axis=0)
        .reshape(group_rows, heads_here * HEAD_SIZE)
        .astype(jnp.bfloat16)
    )
    partial_branch = jnp.dot(attention_output, out_weight, preferred_element_type=jnp.float32)
    branch = lax.psum_scatter(
        partial_branch.astype(jnp.bfloat16), "col", scatter_dimension=0, tiled=True
    ).astype(jnp.float32)
    resid = resid_in + branch
    mixer_in, second_pull = jax.vjp(norm_rows, resid, second_gain)
    mixer_low = mixer_in.astype(jnp.bfloat16)
    logits = jnp.dot(mixer_low, router_weight, preferred_element_type=jnp.float32)
    expert_count = router_weight.shape[1]
    chosen = jnp.take_along_axis(logits, routes, axis=1)
    route_weights, route_pull = jax.vjp(route_softmax, chosen)
    capacity = max(2, tok_rows * TOP * 9 // (expert_count * 8))
    flat_routes = routes.reshape(-1)
    target = flat_routes * capacity + slot_numbers(flat_routes, expert_count)
    slot_rows = expert_count * capacity
    outgoing = (
        jnp.zeros((slot_rows, model_width), jnp.bfloat16)
        .at[target]
        .set(jnp.repeat(mixer_low, TOP, axis=0))
    )
    arrived = trade(outgoing.reshape(expert_count, capacity, model_width)).reshape(
        slot_rows, model_width
    )
    gate_value = jnp.dot(arrived, gate_weight[0], preferred_element_type=jnp.float32)
    up_value = jnp.dot(arrived, up_weight[0], preferred_element_type=jnp.float32)
    sigmoid_gate = jax.nn.sigmoid(gate_value)
    activated = (gate_value * sigmoid_gate * up_value).astype(jnp.bfloat16)
    expert_rows = jnp.dot(activated, down_weight[0], preferred_element_type=jnp.float32).astype(
        jnp.bfloat16
    )
    returned = trade(expert_rows.reshape(expert_count, capacity, model_width)).reshape(
        slot_rows, model_width
    )
    expert_out = returned[target].reshape(tok_rows, TOP, model_width)
    mixed = jnp.sum(route_weights[:, :, None] * expert_out, axis=1)
    block_out = (resid + mixed).astype(jnp.bfloat16)
    grad_out = cotangent.astype(jnp.float32)
    grad_expert_out = (
        (route_weights[:, :, None] * grad_out[:, None, :])
        .astype(jnp.bfloat16)
        .reshape(tok_rows * TOP, model_width)
    )
    grad_weights = jnp.sum(expert_out * grad_out[:, None, :], axis=-1)
    outgoing_grad = (
        jnp.zeros((slot_rows, model_width), jnp.bfloat16).at[target].set(grad_expert_out)
    )
    grad_arrived = trade(outgoing_grad.reshape(expert_count, capacity, model_width)).reshape(
        slot_rows, model_width
    )
    grad_act = jnp.einsum(
        "rd,fd->rf", grad_arrived, down_weight[0], preferred_element_type=jnp.float32
    )
    down_grad = jnp.einsum("rf,rd->fd", activated, grad_arrived, preferred_element_type=jnp.float32)
    grad_gate = (
        grad_act * up_value * sigmoid_gate * (1.0 + gate_value * (1.0 - sigmoid_gate))
    ).astype(jnp.bfloat16)
    grad_up = (grad_act * gate_value * sigmoid_gate).astype(jnp.bfloat16)
    gate_grad = jnp.einsum("rd,rf->df", arrived, grad_gate, preferred_element_type=jnp.float32)
    up_grad = jnp.einsum("rd,rf->df", arrived, grad_up, preferred_element_type=jnp.float32)
    grad_rows = jnp.einsum(
        "rf,df->rd", grad_gate, gate_weight[0], preferred_element_type=jnp.float32
    )
    grad_rows = (
        grad_rows
        + jnp.einsum("rf,df->rd", grad_up, up_weight[0], preferred_element_type=jnp.float32)
    ).astype(jnp.bfloat16)
    grad_back = trade(grad_rows.reshape(expert_count, capacity, model_width)).reshape(
        slot_rows, model_width
    )
    grad_mixer = jnp.sum(
        grad_back[target].reshape(tok_rows, TOP, model_width).astype(jnp.float32), axis=1
    )
    (grad_chosen,) = route_pull(grad_weights)
    picks = routes[:, :, None] == jnp.arange(expert_count, dtype=jnp.int32)[None, None, :]
    grad_logits = jnp.sum(jnp.where(picks, grad_chosen[:, :, None], 0.0), axis=1).astype(
        jnp.bfloat16
    )
    router_grad = jnp.einsum(
        "td,te->de", mixer_low, grad_logits, preferred_element_type=jnp.float32
    )
    grad_mixer = grad_mixer + jnp.einsum(
        "te,de->td", grad_logits, router_weight, preferred_element_type=jnp.float32
    )
    grad_second, second_gain_grad = second_pull(grad_mixer)
    grad_resid = grad_out + grad_second
    grad_branch = lax.all_gather(grad_resid.astype(jnp.bfloat16), "col", axis=0, tiled=True)
    out_grad = jnp.einsum(
        "gf,gd->fd", attention_output, grad_branch, preferred_element_type=jnp.float32
    )
    grad_attended = (
        jnp.einsum("gd,fd->gf", grad_branch, out_weight, preferred_element_type=jnp.float32)
        .astype(jnp.bfloat16)
        .reshape(group_rows, heads_here, HEAD_SIZE)
    )
    query_grads = []
    key_grad = jnp.zeros((group_rows, HEAD_SIZE), jnp.float32)
    value_grad = jnp.zeros((group_rows, HEAD_SIZE), jnp.float32)
    for block_index, row_begin in enumerate(range(0, group_rows, block_rows)):
        row_end = row_begin + block_rows
        scores = (
            jnp.einsum(
                "qhd,kd->hqk",
                query_low[row_begin:row_end],
                key_low[:row_end],
                preferred_element_type=jnp.float32,
            )
            * score_scale
        )
        scores = jnp.where(allowed_block(segment_row, row_begin, row_end)[None], scores, NEGATIVE)
        softmax_full = jnp.exp(scores - log_totals[block_index])
        softmax_low = softmax_full.astype(jnp.bfloat16)
        grad_soft = jnp.einsum(
            "qhd,kd->hqk",
            grad_attended[row_begin:row_end],
            value_lowered[:row_end],
            preferred_element_type=jnp.float32,
        )
        grad_scores = (
            softmax_full * (grad_soft - jnp.sum(softmax_full * grad_soft, axis=-1, keepdims=True))
        ).astype(jnp.bfloat16)
        query_grads.append(
            jnp.einsum(
                "hqk,kd->qhd", grad_scores, key_low[:row_end], preferred_element_type=jnp.float32
            )
            * score_scale
        )
        key_grad = key_grad.at[:row_end].add(
            jnp.einsum(
                "hqk,qhd->kd",
                grad_scores,
                query_low[row_begin:row_end],
                preferred_element_type=jnp.float32,
            )
            * score_scale
        )
        value_grad = value_grad.at[:row_end].add(
            jnp.einsum(
                "hqk,qhd->kd",
                softmax_low,
                grad_attended[row_begin:row_end],
                preferred_element_type=jnp.float32,
            )
        )
    grad_query_raw, query_gain_grad = query_pull(jnp.concatenate(query_grads, axis=0))
    grad_key_raw, key_gain_grad = key_pull(key_grad[:, None, :])
    query_grad_low = grad_query_raw.reshape(group_rows, heads_here * HEAD_SIZE).astype(jnp.bfloat16)
    key_grad_low = grad_key_raw[:, 0, :].astype(jnp.bfloat16)
    value_grad_low = value_grad.astype(jnp.bfloat16)
    grad_normed_part = jnp.einsum(
        "gf,df->gd", query_grad_low, query_weight, preferred_element_type=jnp.float32
    )
    grad_normed_part = grad_normed_part + jnp.einsum(
        "gf,df->gd", key_grad_low, key_columns, preferred_element_type=jnp.float32
    )
    grad_normed_part = grad_normed_part + jnp.einsum(
        "gf,df->gd", value_grad_low, value_columns, preferred_element_type=jnp.float32
    )
    grad_normed = lax.psum_scatter(
        grad_normed_part.astype(jnp.bfloat16), "col", scatter_dimension=0, tiled=True
    ).astype(jnp.float32)
    grad_first, first_gain_grad = first_pull(grad_normed)
    input_grad = (grad_resid + grad_first).astype(jnp.bfloat16)
    query_grad = jnp.einsum(
        "gd,gf->df", gathered, query_grad_low, preferred_element_type=jnp.float32
    )
    key_head_grad = jnp.einsum(
        "gd,gf->df", gathered, key_grad_low, preferred_element_type=jnp.float32
    )
    value_head_grad = jnp.einsum(
        "gd,gf->df", gathered, value_grad_low, preferred_element_type=jnp.float32
    )
    key_weight_part = place_head(key_head_grad, key_projection.shape, kv_start)
    value_weight_part = place_head(value_head_grad, value_projection.shape, kv_start)
    query_grad, out_grad = (
        lax.psum(query_grad.astype(jnp.bfloat16), "row").astype(jnp.float32),
        lax.psum(out_grad.astype(jnp.bfloat16), "row").astype(jnp.float32),
    )
    (
        router_grad,
        key_weight_part,
        value_weight_part,
        first_gain_grad,
        second_gain_grad,
        query_gain_grad,
        key_gain_grad,
    ) = lax.psum(
        (
            router_grad,
            key_weight_part,
            value_weight_part,
            first_gain_grad,
            second_gain_grad,
            query_gain_grad,
            key_gain_grad,
        ),
        ("row", "col"),
    )
    return (
        block_out,
        input_grad,
        first_gain_grad,
        query_grad,
        key_weight_part,
        value_weight_part,
        out_grad,
        query_gain_grad,
        key_gain_grad,
        second_gain_grad,
        router_grad,
        gate_grad[None],
        up_grad[None],
        down_grad[None],
    )


def solution(mesh):
    placed = (
        P(("row", "col"), None),
        P(),
        P(None, "col"),
        P(),
        P(),
        P("col", None),
        P(),
        P(),
        P(),
        P(),
        P(("row", "col"), None, None),
        P(("row", "col"), None, None),
        P(("row", "col"), None, None),
        P("row", None),
        P(("row", "col"), None),
        P(("row", "col"), None),
    )
    return jax.shard_map(
        shards,
        mesh=mesh,
        in_specs=placed,
        out_specs=(
            P(("row", "col"), None),
            P(("row", "col"), None),
            P(),
            P(None, "col"),
            P(),
            P(),
            P("col", None),
            P(),
            P(),
            P(),
            P(),
            P(("row", "col"), None, None),
            P(("row", "col"), None, None),
            P(("row", "col"), None, None),
        ),
        check_vma=False,
    )
```

profile of v0, /device:TPU:0, one launch (start us, length us, event | category | flops | bytes accessed | tf_op | source)
XLA Modules:
  0.0 1155.9 jit_solution(15615479029955595789)
XLA Ops:
  16.9 43.5 %all-gather.3.cloned.1.call-done = bf16[512,2048]{1,0:T(8,128)(2,1)} async-done(((bf16[128,2048]{1,0:T(8,128)(2,1)}), bf16[512,2048]{1,0:T(8,128)(2,1)}) %all-gather.3.cloned.1.call-update) | async-done | bytes 2097168 | tf_op jit(solution)/shard_map/all_gather | solution.py:96
  60.4 5.1 fusion.109
  69.8 2.7 multiply_reduce_fusion.5
  75.7 2.2 fusion.108
  86.0 3.7 convolution_convert_fusion.3
  90.3 9.0 reduce-window.19
  99.8 32.6 %reduce-scatter.3.cloned.1.call-done = bf16[128,2048]{1,0:T(8,128)(2,1)} async-done(((bf16[512,2048]{1,0:T(8,128)(2,1)}), bf16[128,2048]{1,0:T(8,128)(2,1)}) %reduce-scatter.3.cloned.1.call-update) | async-done | bytes 524304 | tf_op jit(solution)/shard_map/reduce_scatter | solution.py:154
  133.9 2.2 multiply_convert_fusion.3
  136.1 10.2 scatter_custom_fusion
  146.4 7.2 reshape.557
  153.5 3.9 all-to-all-start
  161.1 7.0 gather_fusion.2
  168.6 10.2 scatter_custom_fusion.1
  178.8 7.2 reshape.561
  186.0 85.9 %all-to-all-done = bf16[32,36,2048]{2,1,0:T(8,128)(2,1)} async-done(((bf16[32,36,2048]{2,1,0:T(8,128)(2,1)}), bf16[32,36,2048]{2,1,0:T(8,128)(2,1)}, u32[]{:S(2)}, u32[]{:S(2)}) %all-to-all-start) | async-done | bytes 4718624 | tf_op jit(solution)/shard_map/all_to_all | solution.py:70
  271.9 6.5 all-to-all-start.2
  278.4 7.2 reshape.558
  285.6 9.1 fusion.26
  294.7 5.7 fusion.22
  300.4 92.4 %all-to-all-done.2 = bf16[32,36,2048]{2,1,0:T(8,128)(2,1)} async-done(((bf16[32,36,2048]{2,1,0:T(8,128)(2,1)}), bf16[32,36,2048]{2,1,0:T(8,128)(2,1)}, u32[]{:S(2)}, u32[]{:S(2)}) %all-to-all-start.2) | async-done | bytes 4718624 | tf_op jit(solution)/shard_map/all_to_all | solution.py:70
  392.8 7.2 reshape.562
  400.1 9.6 multiply_convert_fusion
  409.7 3.9 fusion.24
  413.6 6.0 add_convert_fusion
  419.6 7.2 reshape.563
  426.7 6.4 all-to-all-start.3
  433.1 6.9 convolution_convert_fusion
  440.0 7.2 reshape.559
  447.2 100.3 %all-to-all-done.3 = bf16[32,36,2048]{2,1,0:T(8,128)(2,1)} async-done(((bf16[32,36,2048]{2,1,0:T(8,128)(2,1)}), bf16[32,36,2048]{2,1,0:T(8,128)(2,1)}, u32[]{:S(2)}, u32[]{:S(2)}) %all-to-all-start.3) | async-done | bytes 4718624 | tf_op jit(solution)/shard_map/all_to_all | solution.py:70
  547.5 6.4 all-to-all-start.1
  553.9 7.2 reshape.564
  561.2 11.8 %gather_fusion.1 = bf16[1024,2048]{1,0:T(8,128)(2,1)} fusion(bf16[1152,2048]{1,0:T(8,128)(2,1)} %reshape.564, s32[1024]{0:T(1024)S(1)} %broadcast_clamp_fusion), kind=kCustom, calls=%fused_computation.1 | custom fusion | bytes 8392704 | tf_op jit(solution)/shard_map/gather | solution.py:223
  572.9 6.0 convert_reduce_fusion
  578.9 89.3 %all-to-all-done.1 = bf16[32,36,2048]{2,1,0:T(8,128)(2,1)} async-done(((bf16[32,36,2048]{2,1,0:T(8,128)(2,1)}), bf16[32,36,2048]{2,1,0:T(8,128)(2,1)}, u32[]{:S(2)}, u32[]{:S(2)}) %all-to-all-start.1) | async-done | bytes 4718624 | tf_op jit(solution)/shard_map/all_to_all | solution.py:70
  668.3 7.2 reshape.560
  675.5 11.8 %gather_fusion = bf16[1024,2048]{1,0:T(8,128)(2,1)} fusion(bf16[1152,2048]{1,0:T(8,128)(2,1)} %reshape.560, s32[1024]{0:T(1024)S(1)} %broadcast_clamp_fusion), kind=kCustom, calls=%fused_computation | custom fusion | bytes 8392704 | tf_op jit(solution)/shard_map/gather | solution.py:186
  687.3 5.9 fusion.1
  693.5 2.4 multiply_reduce_fusion.2
  697.5 47.2 %all-gather.5.cloned.1.call-done = bf16[512,2048]{1,0:T(8,128)(2,1)} async-done(((bf16[128,2048]{1,0:T(8,128)(2,1)}), bf16[512,2048]{1,0:T(8,128)(2,1)}) %all-gather.5.cloned.1.call-update) | async-done | bytes 2097168 | tf_op jit(solution)/shard_map/all_gather | solution.py:238
  744.7 5.3 fusion.35
  750.1 5.7 fusion.2
  755.8 2.6 fusion.4
  761.9 2.3 multiply_reduce_fusion
  764.3 2.8 fusion.30
  767.0 2.3 copy.195
  769.3 6.3 convolution_convert_fusion.1
  775.6 4.4 convolution_convert_fusion.2
  780.4 4.7 fusion.39
  788.4 5.0 fusion.43
  793.5 2.4 fusion.111
  795.9 3.2 add_convert_fusion.1
  801.4 2.5 broadcast.413.clone
  805.7 2.6 broadcast.413.clone.1
  811.5 8.7 convolution_bitcast_fusion.2
  820.2 8.6 convolution_bitcast_fusion.1
  828.9 8.5 convolution_bitcast_fusion
  837.4 67.9 %all-reduce.12.cloned.1.call-done = (bf16[2048,1024]{1,0:T(8,128)(2,1)}, bf16[1024,2048]{1,0:T(8,128)(2,1)}) async-done(((bf16[2048,1024]{1,0:T(8,128)(2,1)}, bf16[1024,2048]{1,0:T(8,128)(2,1)}), (bf16[2048,1024]{1,0:T(8,128)(2,1)}, bf16[1024,2048]{1,0:T(8,128)(2,1)})) %all-reduce.12.cloned.1.call-update) | async-done | bytes 8388624 | tf_op jit(solution)/shard_map/psum | solution.py:327
  905.2 6.8 convert_element_type.186
  912.1 4.4 convert_element_type.188
  916.6 34.6 %reduce-scatter.5.cloned.1.call-done = bf16[128,2048]{1,0:T(8,128)(2,1)} async-done(((bf16[512,2048]{1,0:T(8,128)(2,1)}), bf16[128,2048]{1,0:T(8,128)(2,1)}) %reduce-scatter.5.cloned.1.call-update) | async-done | bytes 524304 | tf_op jit(solution)/shard_map/reduce_scatter | solution.py:310
  952.8 41.5 %all-reduce.4 = (f32[2048]{0:T(1024)}, f32[128]{0:T(128)}, f32[128]{0:T(128)}, f32[2048]{0:T(1024)}) all-reduce(f32[2048]{0:T(1024)S(1)} %get-tuple-element.60, f32[128]{0:T(128)S(1)} %copy-done.72, f32[128]{0:T(128)S(1)} %copy-done.71, f32[2048]{0:T(1024)S(1)} %copy-done.55), channel_id=1, replica_groups=mesh['row'=8,'col'=4] {'row','col'}, use_global_device_ids=true, to_apply=%region_30.31 | all-reduce | flops 4352 | bytes 34816 | tf_op jit(solution)/shard_map/psum | solution.py:338
  994.4 3.2 fusion.51
  997.6 143.4 %all-reduce.10.cloned.1.call-done = (f32[2048,512]{1,0:T(8,128)}, f32[2048,512]{1,0:T(8,128)}, f32[2048,32]{0,1:T(8,128)}) async-done(((f32[2048,512]{1,0:T(8,128)}, f32[2048,512]{1,0:T(8,128)}, f32[2048,32]{0,1:T(8,128)}), (f32[2048,512]{1,0:T(8,128)}, f32[2048,512]{1,0:T(8,128)}, f32[2048,32]{0,1:T(8,128)})) %all-reduce.10.cloned.1.call-update) | async-done | bytes 8650768 | tf_op jit(solution)/shard_map/psum | solution.py:338
  1141.0 4.9 copy.234
  (270 shorter events, 51.9 us)
Async XLA Ops:
  7.2 392.9 %copy-start = (bf16[1,768,2048]{2,1,0:T(8,128)(2,1)S(1)}, bf16[1,768,2048]{2,1,0:T(8,128)(2,1)}, u32[]{:S(2)}) copy-start(bf16[1,768,2048]{2,1,0:T(8,128)(2,1)} %param.36) | copy-start | bytes 9437188
  7.2 53.2 %all-gather.3.cloned.1.call-start = ((), (), s32[]{:S(2)}) async-start(), calls=%async_computation.6 | async-start | bytes 2621440 | tf_op jit(solution)/shard_map/all_gather | solution.py:96
  11.8 120.6 %reduce-scatter.3.cloned.1.call-start = ((), (), s32[]{:S(2)}) async-start(), calls=%async_computation.7 | async-start | bytes 2621440 | tf_op jit(solution)/shard_map/reduce_scatter | solution.py:154
  13.3 59.3 %copy-start.62 = (f32[64]{0:T(128)}, f32[64]{0:T(128)S(1)}, u32[]{:S(2)}) copy-start(f32[64]{0:T(128)S(1)} %multiply_power_fusion) | copy-start | bytes 772
  13.5 59.1 %copy-start.50 = (f32[512]{0:T(512)}, f32[512]{0:T(512)S(1)}, u32[]{:S(2)}) copy-start(f32[512]{0:T(512)S(1)} %fusion.94) | copy-start | bytes 6148
  16.9 57.8 %copy-start.25 = (f32[512,64]{1,0:T(8,128)}, f32[512,64]{1,0:T(8,128)S(1)}, u32[]{:S(2)}) copy-start(f32[512,64]{1,0:T(8,128)S(1)} %get-tuple-element.91) | copy-start | bytes 393220
  67.3 5.2 copy-start.64
  67.3 6.4 copy-start.67
  69.7 5.0 copy-start.40
  69.7 5.0 copy-start.27
  77.9 5.3 copy-start.2
  89.7 44.2 %copy-start.44 = (f32[2048]{0:T(1024)S(1)}, f32[2048]{0:T(1024)}, u32[]{:S(2)}) copy-start(f32[2048]{0:T(1024)} %param.32) | copy-start | bytes 24580
  133.9 562.0 %copy-start.58 = (f32[128]{0:T(128)}, f32[128]{0:T(128)S(1)}, u32[]{:S(2)}) copy-start(f32[128]{0:T(128)S(1)} %fusion.101) | copy-start | bytes 1540
  153.5 6.3 copy-start.36
  153.5 118.3 %all-to-all-start = ((bf16[32,36,2048]{2,1,0:T(8,128)(2,1)}), bf16[32,36,2048]{2,1,0:T(8,128)(2,1)}, u32[]{:S(2)}, u32[]{:S(2)}) async-start(bf16[32,36,2048]{2,1,0:T(8,128)(2,1)} %reshape.557), calls=%async_computation.1 | async-start | bytes 10485760 | tf_op jit(solution)/shard_map/all_to_all | solution.py:70
  271.9 120.9 %all-to-all-start.2 = ((bf16[32,36,2048]{2,1,0:T(8,128)(2,1)}), bf16[32,36,2048]{2,1,0:T(8,128)(2,1)}, u32[]{:S(2)}, u32[]{:S(2)}) async-start(bf16[32,36,2048]{2,1,0:T(8,128)(2,1)} %reshape.561), calls=%async_computation.3 | async-start | bytes 10485760 | tf_op jit(solution)/shard_map/all_to_all | solution.py:70
  285.6 9.1 copy-start.18
  285.6 9.1 copy-start.78
  400.0 9.6 copy-start.77
  426.7 120.8 %all-to-all-start.3 = ((bf16[32,36,2048]{2,1,0:T(8,128)(2,1)}), bf16[32,36,2048]{2,1,0:T(8,128)(2,1)}, u32[]{:S(2)}, u32[]{:S(2)}) async-start(bf16[32,36,2048]{2,1,0:T(8,128)(2,1)} %reshape.563), calls=%async_computation.4 | async-start | bytes 10485760 | tf_op jit(solution)/shard_map/all_to_all | solution.py:70
  547.5 120.8 %all-to-all-start.1 = ((bf16[32,36,2048]{2,1,0:T(8,128)(2,1)}), bf16[32,36,2048]{2,1,0:T(8,128)(2,1)}, u32[]{:S(2)}, u32[]{:S(2)}) async-start(bf16[32,36,2048]{2,1,0:T(8,128)(2,1)} %reshape.559), calls=%async_computation.2 | async-start | bytes 10485760 | tf_op jit(solution)/shard_map/all_to_all | solution.py:70
  553.9 190.8 %all-gather.5.cloned.1.call-start = ((), (), s32[]{:S(2)}) async-start(), calls=%async_computation.8 | async-start | bytes 2621440 | tf_op jit(solution)/shard_map/all_gather | solution.py:238
  675.5 11.8 %copy-start.13 = (f32[128,2048]{1,0:T(8,128)S(1)}, f32[128,2048]{1,0:T(8,128)}, u32[]{:S(2)}) copy-start(f32[128,2048]{1,0:T(8,128)} %convert_element_type.164) | copy-start | bytes 3145732
  687.3 6.2 copy-start.9
  687.3 6.2 copy-start.10
  687.3 8.6 copy-start.16
  693.5 56.5 %copy-start.48 = (bf16[128,32]{0,1:T(8,128)(2,1)}, bf16[128,32]{0,1:T(8,128)(2,1)S(1)}, u32[]{:S(2)}) copy-start(bf16[128,32]{0,1:T(8,128)(2,1)S(1)} %select_reduce_fusion) | copy-start | bytes 24580
  695.9 54.1 %copy-start.11 = (f32[128,2048]{1,0:T(8,128)}, f32[128,2048]{1,0:T(8,128)S(1)}, u32[]{:S(2)}) copy-start(f32[128,2048]{1,0:T(8,128)S(1)} %get-tuple-element.97) | copy-start | bytes 3145732
  695.9 54.1 %copy-start.69 = (f32[128]{0:T(128)}, f32[128]{0:T(128)S(1)}, u32[]{:S(2)}) copy-start(f32[128]{0:T(128)S(1)} %multiply_multiply_fusion.3) | copy-start | bytes 1540
  697.2 208.0 %all-reduce.12.cloned.1.call-start = ((), (), s32[]{:S(2)}) async-start(), calls=%async_computation.11 | async-start | bytes 16777216 | tf_op jit(solution)/shard_map/psum | solution.py:327
  697.5 52.6 %copy-start.43 = (bf16[512,128,1]{1,0,2:T(8,128)(2,1)S(1)}, bf16[512,128,1]{1,0,2:T(8,128)(2,1)}, u32[]{:S(2)}) copy-start(bf16[512,128,1]{1,0,2:T(8,128)(2,1)} %copy-done.42) | copy-start | bytes 393220
  744.7 11.1 slice-start
  750.1 5.7 copy-start.23
  750.1 5.7 slice-start.1
  769.3 6.3 copy-start.5
  769.3 6.3 copy-start.30
  780.1 5.1 copy-start.51
  780.1 5.1 copy-start.63
  780.1 5.6 copy-start.22
  780.1 5.6 copy-start.53
  780.1 5.6 copy-start.65
  780.1 6.3 copy-start.57
  780.1 171.0 %reduce-scatter.5.cloned.1.call-start = ((), (), s32[]{:S(2)}) async-start(), calls=%async_computation.9 | async-start | bytes 2621440 | tf_op jit(solution)/shard_map/reduce_scatter | solution.py:310
  780.4 6.0 copy-start.54
  780.4 6.0 copy-start.66
  788.4 5.0 copy-start.31
  788.4 5.2 copy-start.76
  799.1 341.8 %all-reduce.10.cloned.1.call-start = ((), (), s32[]{:S(2)}) async-start(), calls=%async_computation.10 | async-start | bytes 17301504 | tf_op jit(solution)/shard_map/psum | solution.py:338
  811.5 8.7 copy-start.85
  820.2 8.6 copy-start.81
  905.2 6.8 copy-start.19
  912.0 39.2 %copy-start.47 = (f32[2048]{0:T(1024)S(1)}, f32[2048]{0:T(1024)}, u32[]{:S(2)}) copy-start(f32[2048]{0:T(1024)} %param.25) | copy-start | bytes 24580
  912.0 39.2 %copy-start.61 = (f32[128]{0:T(128)S(1)}, f32[128]{0:T(128)}, u32[]{:S(2)}) copy-start(f32[128]{0:T(128)} %copy-done.60) | copy-start | bytes 1540
  912.0 40.8 %copy-start.55 = (f32[2048]{0:T(1024)S(1)}, f32[2048]{0:T(1024)}, u32[]{:S(2)}) copy-start(f32[2048]{0:T(1024)} %get-tuple-element.58) | copy-start | bytes 24580
  912.0 40.8 %copy-start.71 = (f32[128]{0:T(128)S(1)}, f32[128]{0:T(128)}, u32[]{:S(2)}) copy-start(f32[128]{0:T(128)} %get-tuple-element.62) | copy-start | bytes 1540
  912.1 40.7 %copy-start.72 = (f32[128]{0:T(128)S(1)}, f32[128]{0:T(128)}, u32[]{:S(2)}) copy-start(f32[128]{0:T(128)} %get-tuple-element.54) | copy-start | bytes 1540
  912.1 82.3 %copy-start.74 = (f32[128]{0:T(128)S(1)}, f32[128]{0:T(128)}, u32[]{:S(2)}) copy-start(f32[128]{0:T(128)} %copy-done.73) | copy-start | bytes 1540
  912.1 82.3 %copy-start.12 = (f32[128,2048]{1,0:T(8,128)S(1)}, f32[128,2048]{1,0:T(8,128)}, u32[]{:S(2)}) copy-start(f32[128,2048]{1,0:T(8,128)} %copy-done.11) | copy-start | bytes 3145732
  912.1 82.3 %copy-start.17 = (bf16[128,2048]{1,0:T(8,128)(2,1)S(1)}, bf16[128,2048]{1,0:T(8,128)(2,1)}, u32[]{:S(2)}) copy-start(bf16[128,2048]{1,0:T(8,128)(2,1)} %param.39) | copy-start | bytes 1572868
  912.1 82.3 %copy-start.45 = (f32[2048]{0:T(1024)S(1)}, f32[2048]{0:T(1024)}, u32[]{:S(2)}) copy-start(f32[2048]{0:T(1024)} %param.32) | copy-start | bytes 24580
  912.1 82.3 %copy-start.59 = (f32[128]{0:T(128)S(1)}, f32[128]{0:T(128)}, u32[]{:S(2)}) copy-start(f32[128]{0:T(128)} %copy-done.58) | copy-start | bytes 1540
  912.1 82.3 %copy-start.70 = (f32[128]{0:T(128)S(1)}, f32[128]{0:T(128)}, u32[]{:S(2)}) copy-start(f32[128]{0:T(128)} %copy-done.69) | copy-start | bytes 1540
  1141.0 4.9 copy-start.20
  1141.0 7.7 copy-start.1
  (34 other events, 78.9 us)
Sparse Core Ops, SparseCore 0:
  11.9 48.3 all-gather.2
  89.9 42.5 reduce-scatter.2
  697.3 47.2 all-gather.4
  780.2 125.0 all-reduce.11
  907.4 43.7 reduce-scatter.4
  958.4 182.5 all-reduce.9
where the time goes:
time: 1160 us
  waiting for transfers between devices  737 us (64%)
  matrix products  134 us (12%)
  local copies, waits for them, and re-layouts  125 us (11%)
  other arithmetic  77.6 us (7%)
  blocking collectives  41.5 us (4%)
  starting transfers between devices  24.1 us (2%)
  between operations  15.9 us (1%)
    all_to_all x4, waiting for transfers between devices, trade(): lax.all_to_all(parcel, ('row', 'col'), split_axis=0, concat_axis=0, tiled...  368 us
    psum x1, waiting for transfers between devices, shards(): lax.psum((router_grad, key_weight_part, value_weight_part, first_gain_gra...  143 us
    psum x1, waiting for transfers between devices, shards(): lax.psum(query_grad.astype(jnp.bfloat16), 'row').astype(jnp.float32)  67.9 us
    all_gather x1, waiting for transfers between devices, shards(): lax.all_gather(grad_resid.astype(jnp.bfloat16), 'col', axis=0, tiled=True)  47.2 us
    all_gather x1, waiting for transfers between devices, shards(): gathered = lax.all_gather(normed_low, 'col', axis=0, tiled=True)  43.5 us
    psum x1, blocking collectives, shards(): lax.psum((router_grad, key_weight_part, value_weight_part, first_gain_gra...  41.5 us
    reduce_scatter x1, waiting for transfers between devices, shards(): lax.psum_scatter(grad_normed_part.astype(jnp.bfloat16), 'col', scatter_di...  34.6 us
    reduce_scatter x1, waiting for transfers between devices, shards(): lax.psum_scatter(partial_branch.astype(jnp.bfloat16), 'col', scatter_dime...  32.6 us
  transfers between devices with their start and end apart: 10, of which 10 were waited for; matrix products, arithmetic and copies ran while one was open for 15% of the time, Pallas kernels for 0%

commit v1 on v0

--- a/solution.py
+++ b/solution.py
@@ -324,7 +324,7 @@
     key_weight_part = place_head(key_head_grad, key_projection.shape, kv_start)
     value_weight_part = place_head(value_head_grad, value_projection.shape, kv_start)
     query_grad, out_grad = (
-        lax.psum(query_grad.astype(jnp.bfloat16), "row").astype(jnp.float32),
+        jnp.sum(lax.all_gather(query_grad.astype(jnp.bfloat16), "row"), axis=0).astype(jnp.float32),
         lax.psum(out_grad.astype(jnp.bfloat16), "row").astype(jnp.float32),
     )
     (

time: 1160 us -> 1280 us (1.10)
  waiting for transfers between devices: 737 us -> 838 us
  other arithmetic: 77.6 us -> 95.1 us
    all_gather x0 -> x1, waiting for transfers between devices: none -> 117 us  [shards(): lax.all_gather(query_grad.astype(jnp.bfloat16), 'row')]
    psum x1, waiting for transfers between devices: 67.9 us -> 21.7 us  [shards(): lax.psum(out_grad.astype(jnp.bfloat16), 'row').astype(jnp.float32)]
    psum x1, waiting for transfers between devices: 143 us -> 169 us  [shards(): lax.psum((router_grad, key_weight_part, value_weight_part, first_gain_gra...]
    reduce_sum x0 -> x1, other arithmetic: none -> 14.5 us  [shards(): jnp.sum(lax.all_gather(query_grad.astype(jnp.bfloat16), 'row'), axis=0)]
  transfers between devices with their start and end apart: 10 -> 11, of which waited for: 10 -> 11; matrix products, arithmetic and copies ran while one was open for 15% -> 15% of each run, Pallas kernels for 0% -> 0%
where the time goes in v1:
time: 1280 us; the launch traced here: 1270 us
  waiting for transfers between devices  838 us (65%)
  matrix products  134 us (10%)
  local copies, waits for them, and re-layouts  126 us (10%)
  other arithmetic  95.1 us (7%)
  blocking collectives  40.9 us (3%)
  starting transfers between devices  24.1 us (2%)
  between operations  15.9 us (1%)
    all_to_all x4, waiting for transfers between devices, trade(): lax.all_to_all(parcel, ('row', 'col'), split_axis=0, concat_axis=0, tiled...  368 us
    psum x1, waiting for transfers between devices, shards(): lax.psum((router_grad, key_weight_part, value_weight_part, first_gain_gra...  169 us
    all_gather x1, waiting for transfers between devices, shards(): lax.all_gather(query_grad.astype(jnp.bfloat16), 'row')  117 us
    all_gather x1, waiting for transfers between devices, shards(): lax.all_gather(grad_resid.astype(jnp.bfloat16), 'col', axis=0, tiled=True)  47.2 us
    all_gather x1, waiting for transfers between devices, shards(): gathered = lax.all_gather(normed_low, 'col', axis=0, tiled=True)  43.5 us
    psum x1, blocking collectives, shards(): lax.psum((router_grad, key_weight_part, value_weight_part, first_gain_gra...  40.9 us
    reduce_scatter x1, waiting for transfers between devices, shards(): lax.psum_scatter(grad_normed_part.astype(jnp.bfloat16), 'col', scatter_di...  39.2 us
    reduce_scatter x1, waiting for transfers between devices, shards(): lax.psum_scatter(partial_branch.astype(jnp.bfloat16), 'col', scatter_dime...  32.6 us
  transfers between devices with their start and end apart: 11, of which 11 were waited for; matrix products, arithmetic and copies ran while one was open for 15% of the time, Pallas kernels for 0%

profile of v1, /device:TPU:0, one launch (start us, length us, event | category | flops | bytes accessed | tf_op | source)
XLA Modules:
  0.0 1273.6 jit_solution(1445782385569337055)
XLA Ops:
  16.8 43.5 %all-gather.5.cloned.1.call-done = bf16[512,2048]{1,0:T(8,128)(2,1)} async-done(((bf16[128,2048]{1,0:T(8,128)(2,1)}), bf16[512,2048]{1,0:T(8,128)(2,1)}) %all-gather.5.cloned.1.call-update) | async-done | bytes 2097168 | tf_op jit(solution)/shard_map/all_gather | solution.py:96
  60.3 5.1 fusion.109
  69.7 2.7 multiply_reduce_fusion.5
  86.0 3.7 convolution_convert_fusion.3
  90.2 9.0 reduce-window.19
  99.7 32.6 %reduce-scatter.3.cloned.1.call-done = bf16[128,2048]{1,0:T(8,128)(2,1)} async-done(((bf16[512,2048]{1,0:T(8,128)(2,1)}), bf16[128,2048]{1,0:T(8,128)(2,1)}) %reduce-scatter.3.cloned.1.call-update) | async-done | bytes 524304 | tf_op jit(solution)/shard_map/reduce_scatter | solution.py:154
  136.1 10.2 scatter_custom_fusion
  146.3 7.2 reshape.557
  153.5 3.9 all-to-all-start
  161.0 7.0 gather_fusion.2
  168.5 10.2 scatter_custom_fusion.1
  178.7 7.2 reshape.561
  185.8 85.9 %all-to-all-done = bf16[32,36,2048]{2,1,0:T(8,128)(2,1)} async-done(((bf16[32,36,2048]{2,1,0:T(8,128)(2,1)}), bf16[32,36,2048]{2,1,0:T(8,128)(2,1)}, u32[]{:S(2)}, u32[]{:S(2)}) %all-to-all-start) | async-done | bytes 4718624 | tf_op jit(solution)/shard_map/all_to_all | solution.py:70
  271.8 6.5 all-to-all-start.2
  278.3 7.2 reshape.558
  285.5 9.1 fusion.26
  294.6 5.7 fusion.22
  300.3 92.4 %all-to-all-done.2 = bf16[32,36,2048]{2,1,0:T(8,128)(2,1)} async-done(((bf16[32,36,2048]{2,1,0:T(8,128)(2,1)}), bf16[32,36,2048]{2,1,0:T(8,128)(2,1)}, u32[]{:S(2)}, u32[]{:S(2)}) %all-to-all-start.2) | async-done | bytes 4718624 | tf_op jit(solution)/shard_map/all_to_all | solution.py:70
  392.7 7.2 reshape.562
  399.9 9.6 multiply_convert_fusion
  409.5 3.9 fusion.24
  413.4 6.0 add_convert_fusion
  419.4 7.2 reshape.563
  426.6 6.4 all-to-all-start.3
  432.9 6.9 convolution_convert_fusion
  439.9 7.2 reshape.559
  447.0 100.3 %all-to-all-done.3 = bf16[32,36,2048]{2,1,0:T(8,128)(2,1)} async-done(((bf16[32,36,2048]{2,1,0:T(8,128)(2,1)}), bf16[32,36,2048]{2,1,0:T(8,128)(2,1)}, u32[]{:S(2)}, u32[]{:S(2)}) %all-to-all-start.3) | async-done | bytes 4718624 | tf_op jit(solution)/shard_map/all_to_all | solution.py:70
  547.3 6.4 all-to-all-start.1
  553.8 7.2 reshape.564
  561.0 11.8 gather_fusion.1
  572.8 6.0 convert_reduce_fusion
  578.8 89.3 %all-to-all-done.1 = bf16[32,36,2048]{2,1,0:T(8,128)(2,1)} async-done(((bf16[32,36,2048]{2,1,0:T(8,128)(2,1)}), bf16[32,36,2048]{2,1,0:T(8,128)(2,1)}, u32[]{:S(2)}, u32[]{:S(2)}) %all-to-all-start.1) | async-done | bytes 4718624 | tf_op jit(solution)/shard_map/all_to_all | solution.py:70
  668.1 7.2 reshape.560
  675.3 11.8 gather_fusion
  687.2 5.9 fusion.1
  693.3 2.4 multiply_reduce_fusion.2
  697.3 47.2 %all-gather.7.cloned.1.call-done = bf16[512,2048]{1,0:T(8,128)(2,1)} async-done(((bf16[128,2048]{1,0:T(8,128)(2,1)}), bf16[512,2048]{1,0:T(8,128)(2,1)}) %all-gather.7.cloned.1.call-update) | async-done | bytes 2097168 | tf_op jit(solution)/shard_map/all_gather | solution.py:238
  744.5 5.3 fusion.35
  749.9 5.7 fusion.2
  755.7 2.6 fusion.4
  760.2 2.6 fusion.39
  764.4 2.3 multiply_reduce_fusion
  766.8 2.8 fusion.30
  769.6 2.3 copy.195
  774.1 6.2 convolution_convert_fusion.1
  782.9 5.6 fusion.43
  788.6 2.4 fusion.111
  791.0 3.3 add_convert_fusion.1
  794.3 5.6 convolution_convert_fusion.2
  802.6 2.5 broadcast.413.clone
  806.9 2.5 broadcast.413.clone.1
  812.7 8.5 convolution_bitcast_fusion.2
  821.2 8.5 convolution_bitcast_fusion.1
  829.8 8.5 convolution_bitcast_fusion
  838.4 21.7 %all-reduce.9.cloned.1.call-done = bf16[1024,2048]{1,0:T(8,128)(2,1)} async-done(((bf16[1024,2048]{1,0:T(8,128)(2,1)}), bf16[1024,2048]{1,0:T(8,128)(2,1)}) %all-reduce.9.cloned.1.call-update) | async-done | bytes 4194320 | tf_op jit(solution)/shard_map/psum | solution.py:328
  860.1 6.7 convert_element_type.190
  866.8 39.2 %reduce-scatter.5.cloned.1.call-done = bf16[128,2048]{1,0:T(8,128)(2,1)} async-done(((bf16[512,2048]{1,0:T(8,128)(2,1)}), bf16[128,2048]{1,0:T(8,128)(2,1)}) %reduce-scatter.5.cloned.1.call-update) | async-done | bytes 524304 | tf_op jit(solution)/shard_map/reduce_scatter | solution.py:310
  907.6 40.9 %all-reduce.4 = (f32[2048]{0:T(1024)}, f32[128]{0:T(128)}, f32[128]{0:T(128)}, f32[2048]{0:T(1024)}) all-reduce(f32[2048]{0:T(1024)S(1)} %get-tuple-element.60, f32[128]{0:T(128)S(1)} %copy-done.71, f32[128]{0:T(128)S(1)} %copy-done.70, f32[2048]{0:T(1024)S(1)} %copy-done.54), channel_id=1, replica_groups=mesh['row'=8,'col'=4] {'row','col'}, use_global_device_ids=true, to_apply=%region_30.31 | all-reduce | flops 4352 | bytes 34816 | tf_op jit(solution)/shard_map/psum | solution.py:338
  948.6 3.2 fusion.51
  951.8 117.2 %all-gather.9.cloned.1.call-done = bf16[16384,1024]{1,0:T(8,128)(2,1)} async-done(((bf16[2048,1024]{1,0:T(8,128)(2,1)}), bf16[16384,1024]{1,0:T(8,128)(2,1)}) %all-gather.9.cloned.1.call-update) | async-done | bytes 33554448 | tf_op jit(solution)/shard_map/all_gather | solution.py:327
  1068.9 14.5 %reduce_sum.282 = bf16[2048,1024]{1,0:T(8,128)(2,1)} reduce(bf16[8,2048,1024]{2,1,0:T(8,128)(2,1)} %bitcast.203, bf16[]{:T(256)} %constant.168.clone.1), dimensions={0}, to_apply=%region_31.32 | reduce | flops 14680064 | bytes 37748736 | tf_op jit(solution)/shard_map/reduce_sum | solution.py:327
  1083.5 6.6 convert_element_type.188
  1090.1 168.5 %all-reduce.11.cloned.1.call-done = (f32[2048,512]{1,0:T(8,128)}, f32[2048,512]{1,0:T(8,128)}, f32[2048,32]{0,1:T(8,128)}) async-done(((f32[2048,512]{1,0:T(8,128)}, f32[2048,512]{1,0:T(8,128)}, f32[2048,32]{0,1:T(8,128)}), (f32[2048,512]{1,0:T(8,128)}, f32[2048,512]{1,0:T(8,128)}, f32[2048,32]{0,1:T(8,128)})) %all-reduce.11.cloned.1.call-update) | async-done | bytes 8650768 | tf_op jit(solution)/shard_map/psum | solution.py:338
  1258.6 4.9 copy.233
  (272 shorter events, 57.9 us)
Async XLA Ops:
  7.2 392.7 %copy-start = (bf16[1,768,2048]{2,1,0:T(8,128)(2,1)S(1)}, bf16[1,768,2048]{2,1,0:T(8,128)(2,1)}, u32[]{:S(2)}) copy-start(bf16[1,768,2048]{2,1,0:T(8,128)(2,1)} %param.36) | copy-start | bytes 9437188
  7.2 53.1 %all-gather.5.cloned.1.call-start = ((), (), s32[]{:S(2)}) async-start(), calls=%async_computation.6 | async-start | bytes 2621440 | tf_op jit(solution)/shard_map/all_gather | solution.py:96
  11.8 120.6 %reduce-scatter.3.cloned.1.call-start = ((), (), s32[]{:S(2)}) async-start(), calls=%async_computation.7 | async-start | bytes 2621440 | tf_op jit(solution)/shard_map/reduce_scatter | solution.py:154
  13.2 59.3 %copy-start.61 = (f32[64]{0:T(128)}, f32[64]{0:T(128)S(1)}, u32[]{:S(2)}) copy-start(f32[64]{0:T(128)S(1)} %multiply_power_fusion) | copy-start | bytes 772
  13.4 59.1 %copy-start.52 = (f32[512]{0:T(512)}, f32[512]{0:T(512)S(1)}, u32[]{:S(2)}) copy-start(f32[512]{0:T(512)S(1)} %fusion.94) | copy-start | bytes 6148
  16.8 57.8 %copy-start.25 = (f32[512,64]{1,0:T(8,128)}, f32[512,64]{1,0:T(8,128)S(1)}, u32[]{:S(2)}) copy-start(f32[512,64]{1,0:T(8,128)S(1)} %get-tuple-element.89) | copy-start | bytes 393220
  67.3 5.1 copy-start.63
  67.3 6.3 copy-start.66
  69.7 4.9 copy-start.39
  69.7 4.0 copy-start.6
  69.7 3.9 copy-start.36
  69.7 4.9 copy-start.27
  77.8 5.3 copy-start.2
  89.7 44.2 %copy-start.43 = (f32[2048]{0:T(1024)S(1)}, f32[2048]{0:T(1024)}, u32[]{:S(2)}) copy-start(f32[2048]{0:T(1024)} %param.32) | copy-start | bytes 24580
  133.8 561.9 %copy-start.57 = (f32[128]{0:T(128)}, f32[128]{0:T(128)S(1)}, u32[]{:S(2)}) copy-start(f32[128]{0:T(128)S(1)} %fusion.101) | copy-start | bytes 1540
  153.5 6.2 copy-start.35
  153.5 118.3 %all-to-all-start = ((bf16[32,36,2048]{2,1,0:T(8,128)(2,1)}), bf16[32,36,2048]{2,1,0:T(8,128)(2,1)}, u32[]{:S(2)}, u32[]{:S(2)}) async-start(bf16[32,36,2048]{2,1,0:T(8,128)(2,1)} %reshape.557), calls=%async_computation.1 | async-start | bytes 10485760 | tf_op jit(solution)/shard_map/all_to_all | solution.py:70
  271.8 120.9 %all-to-all-start.2 = ((bf16[32,36,2048]{2,1,0:T(8,128)(2,1)}), bf16[32,36,2048]{2,1,0:T(8,128)(2,1)}, u32[]{:S(2)}, u32[]{:S(2)}) async-start(bf16[32,36,2048]{2,1,0:T(8,128)(2,1)} %reshape.561), calls=%async_computation.3 | async-start | bytes 10485760 | tf_op jit(solution)/shard_map/all_to_all | solution.py:70
  285.5 9.1 copy-start.19
  285.5 9.1 copy-start.77
  399.9 9.6 copy-start.76
  409.5 3.9 copy-start.83
  409.5 3.9 copy-start.78
  426.6 120.8 %all-to-all-start.3 = ((bf16[32,36,2048]{2,1,0:T(8,128)(2,1)}), bf16[32,36,2048]{2,1,0:T(8,128)(2,1)}, u32[]{:S(2)}, u32[]{:S(2)}) async-start(bf16[32,36,2048]{2,1,0:T(8,128)(2,1)} %reshape.563), calls=%async_computation.4 | async-start | bytes 10485760 | tf_op jit(solution)/shard_map/all_to_all | solution.py:70
  547.3 120.8 %all-to-all-start.1 = ((bf16[32,36,2048]{2,1,0:T(8,128)(2,1)}), bf16[32,36,2048]{2,1,0:T(8,128)(2,1)}, u32[]{:S(2)}, u32[]{:S(2)}) async-start(bf16[32,36,2048]{2,1,0:T(8,128)(2,1)} %reshape.559), calls=%async_computation.2 | async-start | bytes 10485760 | tf_op jit(solution)/shard_map/all_to_all | solution.py:70
  553.7 190.8 %all-gather.7.cloned.1.call-start = ((), (), s32[]{:S(2)}) async-start(), calls=%async_computation.8 | async-start | bytes 2621440 | tf_op jit(solution)/shard_map/all_gather | solution.py:238
  675.3 11.8 copy-start.12
  687.2 6.2 copy-start.8
  687.2 6.2 copy-start.9
  687.2 8.6 copy-start.17
  693.3 56.5 %copy-start.47 = (bf16[128,32]{0,1:T(8,128)(2,1)}, bf16[128,32]{0,1:T(8,128)(2,1)S(1)}, u32[]{:S(2)}) copy-start(bf16[128,32]{0,1:T(8,128)(2,1)S(1)} %select_reduce_fusion) | copy-start | bytes 24580
  695.7 54.1 %copy-start.10 = (f32[128,2048]{1,0:T(8,128)}, f32[128,2048]{1,0:T(8,128)S(1)}, u32[]{:S(2)}) copy-start(f32[128,2048]{1,0:T(8,128)S(1)} %get-tuple-element.95) | copy-start | bytes 3145732
  695.7 54.1 %copy-start.68 = (f32[128]{0:T(128)}, f32[128]{0:T(128)S(1)}, u32[]{:S(2)}) copy-start(f32[128]{0:T(128)S(1)} %multiply_multiply_fusion.3) | copy-start | bytes 1540
  697.1 163.1 %all-reduce.9.cloned.1.call-start = ((), (), s32[]{:S(2)}) async-start(), calls=%async_computation.10 | async-start | bytes 8388608 | tf_op jit(solution)/shard_map/psum | solution.py:328
  697.3 52.6 %copy-start.42 = (bf16[512,128,1]{1,0,2:T(8,128)(2,1)S(1)}, bf16[512,128,1]{1,0,2:T(8,128)(2,1)}, u32[]{:S(2)}) copy-start(bf16[512,128,1]{1,0,2:T(8,128)(2,1)} %copy-done.41) | copy-start | bytes 393220
  744.5 11.1 slice-start
  749.9 5.7 copy-start.23
  749.9 5.7 slice-start.1
  766.7 5.1 copy-start.53
  766.8 5.1 copy-start.62
  766.8 6.6 copy-start.22
  766.8 6.6 copy-start.50
  766.8 6.6 copy-start.64
  766.8 7.3 copy-start.56
  780.3 125.6 %reduce-scatter.5.cloned.1.call-start = ((), (), s32[]{:S(2)}) async-start(), calls=%async_computation.9 | async-start | bytes 2621440 | tf_op jit(solution)/shard_map/reduce_scatter | solution.py:310
  782.9 5.6 copy-start.30
  782.9 5.7 copy-start.75
  794.3 274.7 %all-gather.9.cloned.1.call-start = ((), (), s32[]{:S(2)}) async-start(), calls=%async_computation.11 | async-start | bytes 37748736 | tf_op jit(solution)/shard_map/all_gather | solution.py:327
  800.0 458.6 %all-reduce.11.cloned.1.call-start = ((), (), s32[]{:S(2)}) async-start(), calls=%async_computation.12 | async-start | bytes 17301504 | tf_op jit(solution)/shard_map/psum | solution.py:338
  812.7 8.5 copy-start.84
  821.2 8.5 copy-start.80
  838.3 67.7 %copy-start.46 = (f32[2048]{0:T(1024)S(1)}, f32[2048]{0:T(1024)}, u32[]{:S(2)}) copy-start(f32[2048]{0:T(1024)} %param.25) | copy-start | bytes 24580
  838.3 67.7 %copy-start.60 = (f32[128]{0:T(128)S(1)}, f32[128]{0:T(128)}, u32[]{:S(2)}) copy-start(f32[128]{0:T(128)} %copy-done.59) | copy-start | bytes 1540
  838.3 69.3 %copy-start.54 = (f32[2048]{0:T(1024)S(1)}, f32[2048]{0:T(1024)}, u32[]{:S(2)}) copy-start(f32[2048]{0:T(1024)} %get-tuple-element.58) | copy-start | bytes 24580
  838.3 69.3 %copy-start.70 = (f32[128]{0:T(128)S(1)}, f32[128]{0:T(128)}, u32[]{:S(2)}) copy-start(f32[128]{0:T(128)} %get-tuple-element.62) | copy-start | bytes 1540
  838.3 69.3 %copy-start.71 = (f32[128]{0:T(128)S(1)}, f32[128]{0:T(128)}, u32[]{:S(2)}) copy-start(f32[128]{0:T(128)} %get-tuple-element.54) | copy-start | bytes 1540
  838.3 110.3 %copy-start.73 = (f32[128]{0:T(128)S(1)}, f32[128]{0:T(128)}, u32[]{:S(2)}) copy-start(f32[128]{0:T(128)} %copy-done.72) | copy-start | bytes 1540
  838.3 110.3 %copy-start.11 = (f32[128,2048]{1,0:T(8,128)S(1)}, f32[128,2048]{1,0:T(8,128)}, u32[]{:S(2)}) copy-start(f32[128,2048]{1,0:T(8,128)} %copy-done.10) | copy-start | bytes 3145732
  838.3 110.3 %copy-start.18 = (bf16[128,2048]{1,0:T(8,128)(2,1)S(1)}, bf16[128,2048]{1,0:T(8,128)(2,1)}, u32[]{:S(2)}) copy-start(bf16[128,2048]{1,0:T(8,128)(2,1)} %param.39) | copy-start | bytes 1572868
  838.3 110.3 %copy-start.44 = (f32[2048]{0:T(1024)S(1)}, f32[2048]{0:T(1024)}, u32[]{:S(2)}) copy-start(f32[2048]{0:T(1024)} %param.32) | copy-start | bytes 24580
  838.4 110.2 %copy-start.58 = (f32[128]{0:T(128)S(1)}, f32[128]{0:T(128)}, u32[]{:S(2)}) copy-start(f32[128]{0:T(128)} %copy-done.57) | copy-start | bytes 1540
  838.4 110.2 %copy-start.69 = (f32[128]{0:T(128)S(1)}, f32[128]{0:T(128)}, u32[]{:S(2)}) copy-start(f32[128]{0:T(128)} %copy-done.68) | copy-start | bytes 1540
  1258.6 4.9 copy-start.20
  1258.6 7.7 copy-start.1
  (34 other events, 66.7 us)
Sparse Core Ops, SparseCore 0:
  11.9 48.3 all-gather.4
  89.8 42.5 reduce-scatter.2
  697.2 47.2 all-gather.6
  780.5 79.6 all-reduce.8
  862.3 43.6 reduce-scatter.4
  908.3 160.5 all-gather.8
  1076.2 182.3 all-reduce.10
